TPU v7x, 8 devices: a whole 2x2x1 slice. The times are simulated.
8 devices in a mesh: fsdp: 2 (over z, y), ep: 4 (over x, core).
Axes of the slice: x: 2, y: 2, z: 1, core: 2. Of those that a mesh axis runs over, the one named last changes fastest.
Arguments:
- x_in: bfloat16 [2, 16384, 896], P(None, ('fsdp', 'ep'))
- dy_out: bfloat16 [2, 16384, 896], P(None, ('fsdp', 'ep'))
- expert_idx: int32 [2, 16384, 8], P(None, ('fsdp', 'ep'))
- gate_prob: float32 [2, 16384, 8], P(None, ('fsdp', 'ep'))
- w_one: bfloat16 [256, 896, 256], P('ep', 'fsdp')
- w_two: bfloat16 [256, 256, 896], P('ep', None, 'fsdp')
- w_three: bfloat16 [256, 896, 256], P('ep', 'fsdp')
Outputs:
- output 1: bfloat16 [2, 16384, 896], P(None, ('fsdp', 'ep'))
- output 2: float32 [2, 16384, 8], P(None, ('fsdp', 'ep'))
- output 3: float32 [256, 896, 256], P('ep', 'fsdp')
- output 4: float32 [256, 256, 896], P('ep', None, 'fsdp')
- output 5: float32 [256, 896, 256], P('ep', 'fsdp')
All inputs are finite; a program needn't handle non-finite values.
Results may differ from a plain program's by a relative error of at most 0.001.
Values are sent between devices in bfloat16 or wider.
A program may use at most 1 GiB of HBM per device.

v0:
```python
import jax
import jax.numpy as jnp
from jax import lax
from jax.sharding import PartitionSpec as P


def capacity_of(tok_rows, top_k, experts):
    return 8 * ((5 * tok_rows * top_k + 32 * experts - 1) // (32 * experts))


def route_tables(ids_flat, experts, capacity):
    n_choice = ids_flat.shape[0]
    one_hot = (ids_flat[:, None] == jnp.arange(experts, dtype=jnp.int32)[None, :]).astype(jnp.int32)
    position = jnp.sum((jnp.cumsum(one_hot, axis=0) - one_hot) * one_hot, axis=1)
    choice_slot = jnp.where(position < capacity, ids_flat * capacity + position, experts * capacity)
    holder = jnp.full((experts * capacity + 1,), n_choice, jnp.int32)
    holder = holder.at[choice_slot].set(jnp.arange(n_choice, dtype=jnp.int32))
    return choice_slot, holder[:experts * capacity]


def to_experts(send_buf):
    arrived = lax.all_to_all(send_buf, 'ep', 0, 2, tiled=True)
    return arrived.reshape(arrived.shape[1:])


def from_experts(row_block):
    arrived = lax.all_to_all(row_block[None], 'ep', 2, 0, tiled=True)
    return arrived.reshape((-1,) + arrived.shape[3:])


def expert_pass(x_rows, dy_rows, gate_rows, w_one, w_two, w_three):
    h_one = jnp.einsum('erd,edf->erf', x_rows, w_one, preferred_element_type=jnp.float32)
    h_three = jnp.einsum('erd,edf->erf', x_rows, w_three, preferred_element_type=jnp.float32)
    sigma_one = jax.nn.sigmoid(h_one)
    silu_one = h_one * sigma_one
    act_bf = (silu_one * h_three).astype(jnp.bfloat16)
    y_rows = jnp.einsum('erf,efd->erd', act_bf, w_two, preferred_element_type=jnp.float32)
    dg_rows = jnp.sum(dy_rows.astype(jnp.float32) * y_rows, axis=2)
    g_rows = (gate_rows[:, :, None] * dy_rows).astype(jnp.bfloat16)
    d_act = jnp.einsum('erd,efd->erf', g_rows, w_two, preferred_element_type=jnp.float32)
    dh_three = (d_act * silu_one).astype(jnp.bfloat16)
    dh_one = (d_act * h_three * sigma_one * (1.0 + h_one * (1.0 - sigma_one))).astype(jnp.bfloat16)
    dx_rows = (jnp.einsum('erf,edf->erd', dh_one, w_one, preferred_element_type=jnp.float32) + jnp.einsum('erf,edf->erd', dh_three, w_three, preferred_element_type=jnp.float32)).astype(jnp.bfloat16)
    gw_one = jnp.einsum('erd,erf->edf', x_rows, dh_one, preferred_element_type=jnp.float32)
    gw_two = jnp.einsum('erf,erd->efd', act_bf, g_rows, preferred_element_type=jnp.float32)
    gw_three = jnp.einsum('erd,erf->edf', x_rows, dh_three, preferred_element_type=jnp.float32)
    return dx_rows, dg_rows, (gw_one, gw_two, gw_three)


def solution(mesh):
    ep_size = mesh.shape['ep']
    tok_spec = P(None, ('fsdp', 'ep'), None)
    spec_edf = P('ep', 'fsdp', None)
    spec_efd = P('ep', None, 'fsdp')

    def local_step(x_in, dy_out, expert_idx, gate_prob, w_one, w_two, w_three):
        micro_count, tok_rows, d_model = x_in.shape
        top_k = expert_idx.shape[2]
        local_experts = w_one.shape[0]
        experts = local_experts * ep_size
        capacity = capacity_of(tok_rows, top_k, experts)
        n_choice = tok_rows * top_k
        full_one = lax.all_gather(w_one, 'fsdp', axis=1, tiled=True)
        full_two = lax.all_gather(w_two, 'fsdp', axis=2, tiled=True)
        full_three = lax.all_gather(w_three, 'fsdp', axis=1, tiled=True)
        zero_row = jnp.zeros((1, d_model), x_in.dtype)
        zero_val = jnp.zeros((1,), jnp.float32)
        send_shape = (ep_size, local_experts, capacity)
        dx_parts = []
        dg_parts = []
        grad_sum = None
        for mb_index in range(micro_count):
            choice_slot, holder = route_tables(expert_idx[mb_index].reshape(n_choice), experts, capacity)
            tok_slot = holder // top_k
            x_send = jnp.concatenate([x_in[mb_index], zero_row], axis=0)[tok_slot]
            dy_send = jnp.concatenate([dy_out[mb_index], zero_row], axis=0)[tok_slot]
            gate_send = jnp.concatenate([gate_prob[mb_index].reshape(n_choice), zero_val])[holder]
            x_rows = to_experts(x_send.reshape(send_shape + (d_model,)))
            dy_rows = to_experts(dy_send.reshape(send_shape + (d_model,)))
            gate_rows = to_experts(gate_send.reshape(send_shape))
            dx_rows, dg_rows, grad_part = expert_pass(x_rows, dy_rows, gate_rows, full_one, full_two, full_three)
            dx_back = jnp.concatenate([from_experts(dx_rows), zero_row], axis=0)
            dg_back = jnp.concatenate([from_experts(dg_rows), zero_val])
            picked = dx_back[choice_slot].reshape(tok_rows, top_k, d_model)
            dx_parts.append(jnp.sum(picked.astype(jnp.float32), axis=1).astype(jnp.bfloat16))
            dg_parts.append(dg_back[choice_slot].reshape(tok_rows, top_k))
            if grad_sum is None:
                grad_sum = grad_part
            else:
                grad_sum = tuple(prev_sum + new_part for prev_sum, new_part in zip(grad_sum, grad_part))
        dw_one = lax.psum_scatter(grad_sum[0], 'fsdp', scatter_dimension=1, tiled=True)
        dw_two = lax.psum_scatter(grad_sum[1], 'fsdp', scatter_dimension=2, tiled=True)
        dw_three = lax.psum_scatter(grad_sum[2], 'fsdp', scatter_dimension=1, tiled=True)
        return jnp.stack(dx_parts), jnp.stack(dg_parts), dw_one, dw_two, dw_three

    return jax.shard_map(local_step, mesh=mesh, in_specs=(tok_spec, tok_spec, tok_spec, tok_spec, spec_edf, spec_efd, spec_edf), out_specs=(tok_spec, tok_spec, spec_edf, spec_efd, spec_edf), check_vma=False)
```

profile of v0, /device:TPU:6, one launch (start us, length us, event | category | flops | bytes accessed | tf_op | source)
XLA Modules:
  0.0 5061.1 jit_solution(7290022514235248166)
XLA Ops:
  59.5 60.4 %scatter_custom_fusion = s32[20481]{0:T(1024)S(1)} fusion(s32[16384]{0:T(1024)S(1)} %bitcast.163, s32[16384]{0:T(1024)S(1)} %iota.19, s32[]{:T(128)} %constant.40.clone.1), kind=kCustom, calls=%fused_computation.98 | custom fusion | bytes 81928 | tf_op jit(solution)/shard_map/scatter | solution.py:17
  120.6 113.0 %gather_fusion = f32[20480]{0:T(1024)S(1)} fusion(f32[16385]{0:T(1024)S(1)} %pad_maximum_fusion.5, s32[20480]{0:T(1024)S(1)} %get-tuple-element.31), kind=kCustom, calls=%fused_computation | custom fusion | bytes 245760 | tf_op jit(solution)/shard_map/gather | solution.py:77
  289.2 60.4 %scatter_custom_fusion.1 = s32[20481]{0:T(1024)S(1)} fusion(s32[16384]{0:T(1024)S(1)} %bitcast.165, s32[16384]{0:T(1024)S(1)} %iota.20, s32[]{:T(128)} %constant.40.clone.1), kind=kCustom, calls=%fused_computation.96 | custom fusion | bytes 81928 | tf_op jit(solution)/shard_map/scatter | solution.py:17
  349.7 113.0 %gather_fusion.4 = f32[20480]{0:T(1024)S(1)} fusion(f32[16385]{0:T(1024)S(1)} %pad_maximum_fusion.4, s32[20480]{0:T(1024)S(1)} %get-tuple-element.33), kind=kCustom, calls=%fused_computation.4 | custom fusion | bytes 245760 | tf_op jit(solution)/shard_map/gather | solution.py:77
  474.6 97.2 %gather_fusion.6 = bf16[20480,896]{1,0:T(8,128)(2,1)} fusion(bf16[2049,896]{1,0:T(8,128)(2,1)} %concatenate.36, s32[20480]{0:T(1024)S(1)} %get-tuple-element.34), kind=kCustom, calls=%fused_computation.6 | custom fusion | bytes 73482240 | tf_op jit(solution)/shard_map/gather | solution.py:75
  587.2 97.2 %gather_fusion.2 = bf16[20480,896]{1,0:T(8,128)(2,1)} fusion(bf16[2049,896]{1,0:T(8,128)(2,1)} %concatenate.32, s32[20480]{0:T(1024)S(1)} %copy-done.2), kind=kCustom, calls=%fused_computation.2 | custom fusion | bytes 73482240 | tf_op jit(solution)/shard_map/gather | solution.py:75
  684.3 293.1 %all-to-all-done.6 = bf16[4,64,80,896]{3,2,1,0:T(8,128)(2,1)} async-done(((bf16[4,64,80,896]{3,2,1,0:T(8,128)(2,1)}), bf16[4,64,80,896]{3,2,1,0:T(8,128)(2,1)}, u32[]{:S(2)}, u32[]{:S(2)}) %all-to-all-start.6) | async-done | bytes 36700192 | tf_op jit(solution)/shard_map/all_to_all | solution.py:22
  997.7 97.2 %gather_fusion.1 = bf16[20480,896]{1,0:T(8,128)(2,1)} fusion(bf16[2049,896]{1,0:T(8,128)(2,1)} %concatenate.31, s32[20480]{0:T(1024)S(1)} %copy-done.2), kind=kCustom, calls=%fused_computation.1 | custom fusion | bytes 73482240 | tf_op jit(solution)/shard_map/gather | solution.py:76
  1094.9 289.0 %all-to-all-done.2 = bf16[4,64,80,896]{3,2,1,0:T(8,128)(2,1)} async-done(((bf16[4,64,80,896]{3,2,1,0:T(8,128)(2,1)}), bf16[4,64,80,896]{3,2,1,0:T(8,128)(2,1)}, u32[]{:S(2)}, u32[]{:S(2)}) %all-to-all-start.2) | async-done | bytes 36700192 | tf_op jit(solution)/shard_map/all_to_all | solution.py:22
  1400.9 97.2 %gather_fusion.5 = bf16[20480,896]{1,0:T(8,128)(2,1)} fusion(bf16[2049,896]{1,0:T(8,128)(2,1)} %concatenate.35, s32[20480]{0:T(1024)S(1)} %copy-done.4), kind=kCustom, calls=%fused_computation.5 | custom fusion | bytes 73482240 | tf_op jit(solution)/shard_map/gather | solution.py:76
  1498.1 292.5 %all-to-all-done.1 = bf16[4,64,80,896]{3,2,1,0:T(8,128)(2,1)} async-done(((bf16[4,64,80,896]{3,2,1,0:T(8,128)(2,1)}), bf16[4,64,80,896]{3,2,1,0:T(8,128)(2,1)}, u32[]{:S(2)}, u32[]{:S(2)}) %all-to-all-start.1) | async-done | bytes 36700192 | tf_op jit(solution)/shard_map/all_to_all | solution.py:22
  1891.7 49.4 copy.113
  1941.1 256.2 %all-to-all-done.5 = bf16[4,64,80,896]{3,2,1,0:T(8,128)(2,1)} async-done(((bf16[4,64,80,896]{3,2,1,0:T(8,128)(2,1)}), bf16[4,64,80,896]{3,2,1,0:T(8,128)(2,1)}, u32[]{:S(2)}, u32[]{:S(2)}) %all-to-all-start.5) | async-done | bytes 36700192 | tf_op jit(solution)/shard_map/all_to_all | solution.py:22
  2233.3 49.4 copy.126
  2564.7 63.4 %convolution_add_fusion.1 = f32[64,256,896]{1,2,0:T(8,128)} fusion(f32[64,256,896]{1,2,0:T(8,128)} %fusion.12, bf16[64,320,256]{2,1,0:T(8,128)(2,1)} %get-tuple-element.18, f32[64,320,896]{2,1,0:T(8,128)} %bitcast.34, f32[64,320]{1,0:T(8,128)S(1)} %copy-done.1), kind=kOutput, calls=%fused_computation.35 | convolution fusion | flops 9446621184 | bytes 201408512 | tf_op jit(solution)/shard_map/erf,erd->efd/dot_general | solution.py:45
  2666.5 52.8 %convolution_add_fusion.2 = f32[64,896,256]{2,1,0:T(8,128)} fusion(f32[64,896,256]{2,1,0:T(8,128)} %fusion.34, bf16[64,320,896]{2,1,0:T(8,128)(2,1)} %bitcast.141, bf16[64,320,256]{2,1,0:T(8,128)(2,1)} %get-tuple-element.19), kind=kOutput, calls=%fused_computation.36 | convolution fusion | flops 9409921024 | bytes 164626432 | tf_op jit(solution)/shard_map/erd,erf->edf/dot_general | solution.py:44
  2757.8 52.8 %convolution_add_fusion = f32[64,896,256]{2,1,0:T(8,128)} fusion(f32[64,896,256]{2,1,0:T(8,128)} %fusion.35, bf16[64,320,896]{2,1,0:T(8,128)(2,1)} %bitcast.142, bf16[64,320,256]{2,1,0:T(8,128)(2,1)} %get-tuple-element.20), kind=kOutput, calls=%fused_computation.34 | convolution fusion | flops 9409921024 | bytes 164626432 | tf_op jit(solution)/shard_map/erd,erf->edf/dot_general | solution.py:46
  3127.6 283.4 %all-to-all-done.7 = bf16[1,64,320,896]{3,1,0,2:T(8,128)(2,1)} async-done(((bf16[1,64,320,896]{3,1,0,2:T(8,128)(2,1)}), bf16[1,64,320,896]{3,1,0,2:T(8,128)(2,1)}, u32[]{:S(2)}, u32[]{:S(2)}) %all-to-all-start.7) | async-done | bytes 36700192 | tf_op jit(solution)/shard_map/all_to_all | solution.py:27
  3426.2 90.5 %gather_fusion.8 = f32[16384]{0:T(1024)S(1)} fusion(f32[20481]{0:T(1024)S(1)} %get-tuple-element.36, s32[16384]{0:T(1024)S(1)} %broadcast_clamp_fusion.1), kind=kCustom, calls=%fused_computation.8 | custom fusion | bytes 196608 | tf_op jit(solution)/shard_map/gather | solution.py:86
  3517.6 90.5 %gather_fusion.9 = f32[16384]{0:T(1024)S(1)} fusion(f32[20481]{0:T(1024)S(1)} %get-tuple-element.35, s32[16384]{0:T(1024)S(1)} %broadcast_clamp_fusion), kind=kCustom, calls=%fused_computation.9 | custom fusion | bytes 196608 | tf_op jit(solution)/shard_map/gather | solution.py:86
  3667.2 598.3 %gather_fusion.7 = bf16[16384,896]{1,0:T(8,128)(2,1)} fusion(bf16[20481,896]{1,0:T(8,128)(2,1)} %concatenate.37, s32[16384]{0:T(1024)S(1)} %broadcast_clamp_fusion), kind=kCustom, calls=%fused_computation.7 | custom fusion | bytes 58785792 | tf_op jit(solution)/shard_map/gather | solution.py:84
  4322.9 594.5 %gather_fusion.3 = bf16[16384,896]{1,0:T(8,128)(2,1)} fusion(bf16[20481,896]{1,0:T(8,128)(2,1)} %concatenate.33, s32[16384]{0:T(1024)S(1)} %copy-done.6), kind=kCustom, calls=%fused_computation.3 | custom fusion | bytes 58785792 | tf_op jit(solution)/shard_map/gather | solution.py:84
  4917.4 65.0 %bitcast_reduce_fusion = bf16[2048,896]{1,0:T(8,128)(2,1)} fusion(bf16[16384,896]{1,0:T(8,128)(2,1)} %gather_fusion.7), kind=kLoop, calls=%fused_computation.22 | loop fusion | flops 12845056 | bytes 33030144 | tf_op jit(solution)/shard_map/reduce_sum | solution.py:85
  4982.4 64.7 %bitcast_reduce_fusion.1 = bf16[2048,896]{1,0:T(8,128)(2,1)} fusion(bf16[16384,896]{1,0:T(8,128)(2,1)} %gather_fusion.3), kind=kLoop, calls=%fused_computation.23 | loop fusion | flops 12845056 | bytes 33030144 | tf_op jit(solution)/shard_map/reduce_sum | solution.py:85
  (174 shorter events, 1125.1 us)
Async XLA Ops:
  59.5 61.1 %copy-start.13 = (s32[16384,1]{0,1:T(1,128)}, s32[16384,1]{0,1:T(1,128)S(1)}, u32[]{:S(2)}) copy-start(s32[16384,1]{0,1:T(1,128)S(1)} %compare_select_fusion.1) | copy-start | bytes 196612
  234.4 229.2 %all-to-all-start = ((f32[4,64,80]{2,1,0:T(8,128)}), f32[4,64,80]{2,1,0:T(8,128)S(1)}, u32[]{:S(2)}, u32[]{:S(2)}) async-start(f32[4,64,80]{2,1,0:T(8,128)} %reshape.177), calls=%async_computation | async-start | bytes 262144 | tf_op jit(solution)/shard_map/all_to_all | solution.py:22
  289.2 173.6 %copy-start.15 = (s32[16384,1]{0,1:T(1,128)}, s32[16384,1]{0,1:T(1,128)S(1)}, u32[]{:S(2)}) copy-start(s32[16384,1]{0,1:T(1,128)S(1)} %compare_select_fusion) | copy-start | bytes 196612
  349.7 124.9 %copy-start.3 = (s32[20480]{0:T(1024)}, s32[20480]{0:T(1024)S(1)}, u32[]{:S(2)}) copy-start(s32[20480]{0:T(1024)S(1)} %get-tuple-element.34) | copy-start | bytes 245764
  463.5 108.2 %copy-start.7 = (f32[4,64,80]{2,1,0:T(8,128)}, f32[4,64,80]{2,1,0:T(8,128)S(1)}, u32[]{:S(2)}) copy-start(f32[4,64,80]{2,1,0:T(8,128)S(1)} %all-to-all-done) | copy-start | bytes 245764
  463.5 108.2 %all-to-all-start.4 = ((f32[4,64,80]{2,1,0:T(8,128)}), f32[4,64,80]{2,1,0:T(8,128)S(1)}, u32[]{:S(2)}, u32[]{:S(2)}) async-start(f32[4,64,80]{2,1,0:T(8,128)} %reshape.184), calls=%async_computation.4 | async-start | bytes 262144 | tf_op jit(solution)/shard_map/all_to_all | solution.py:22
  572.4 405.1 %all-to-all-start.6 = ((bf16[4,64,80,896]{3,2,1,0:T(8,128)(2,1)}), bf16[4,64,80,896]{3,2,1,0:T(8,128)(2,1)}, u32[]{:S(2)}, u32[]{:S(2)}) async-start(bf16[4,64,80,896]{3,2,1,0:T(8,128)(2,1)} %bitcast.146), calls=%async_computation.6 | async-start | bytes 73400320 | tf_op jit(solution)/shard_map/all_to_all | solution.py:22
  977.5 406.4 %all-to-all-start.2 = ((bf16[4,64,80,896]{3,2,1,0:T(8,128)(2,1)}), bf16[4,64,80,896]{3,2,1,0:T(8,128)(2,1)}, u32[]{:S(2)}, u32[]{:S(2)}) async-start(bf16[4,64,80,896]{3,2,1,0:T(8,128)(2,1)} %bitcast.144), calls=%async_computation.2 | async-start | bytes 73400320 | tf_op jit(solution)/shard_map/all_to_all | solution.py:22
  989.3 1293.5 %all-gather.8.cloned.1.call-start = ((), (), s32[]{:S(2)}) async-start(), calls=%async_computation.15 | async-start | bytes 44040192 | tf_op jit(solution)/shard_map/all_gather | solution.py:63
  1383.9 406.7 %all-to-all-start.1 = ((bf16[4,64,80,896]{3,2,1,0:T(8,128)(2,1)}), bf16[4,64,80,896]{3,2,1,0:T(8,128)(2,1)}, u32[]{:S(2)}, u32[]{:S(2)}) async-start(bf16[4,64,80,896]{3,2,1,0:T(8,128)(2,1)} %bitcast.145), calls=%async_computation.1 | async-start | bytes 73400320 | tf_op jit(solution)/shard_map/all_to_all | solution.py:22
  1396.0 917.5 %all-gather.4.cloned.1.call-start = ((), (), s32[]{:S(2)}) async-start(), calls=%async_computation.13 | async-start | bytes 44040192 | tf_op jit(solution)/shard_map/all_gather | solution.py:64
  1790.6 406.7 %all-to-all-start.5 = ((bf16[4,64,80,896]{3,2,1,0:T(8,128)(2,1)}), bf16[4,64,80,896]{3,2,1,0:T(8,128)(2,1)}, u32[]{:S(2)}, u32[]{:S(2)}) async-start(bf16[4,64,80,896]{3,2,1,0:T(8,128)(2,1)} %bitcast.143), calls=%async_computation.5 | async-start | bytes 73400320 | tf_op jit(solution)/shard_map/all_to_all | solution.py:22
  1802.7 551.8 %all-gather.6.cloned.1.call-start = ((), (), s32[]{:S(2)}) async-start(), calls=%async_computation.14 | async-start | bytes 44040192 | tf_op jit(solution)/shard_map/all_gather | solution.py:65
  1803.4 3250.7 %reduce-scatter.6.cloned.1.call-start = ((), (), s32[]{:S(2)}) async-start(), calls=%async_computation.17 | async-start | bytes 88080384 | tf_op jit(solution)/shard_map/reduce_scatter | solution.py:92
  2628.1 2426.0 %reduce-scatter.4.cloned.1.call-start = ((), (), s32[]{:S(2)}) async-start(), calls=%async_computation.16 | async-start | bytes 88080384 | tf_op jit(solution)/shard_map/reduce_scatter | solution.py:91
  2719.4 2334.7 %reduce-scatter.8.cloned.1.call-start = ((), (), s32[]{:S(2)}) async-start(), calls=%async_computation.18 | async-start | bytes 88080384 | tf_op jit(solution)/shard_map/reduce_scatter | solution.py:93
  2848.7 80.5 %all-to-all-start.8 = ((f32[4,1,5120]{2,1,0:T(1,128)}), f32[4,1,5120]{2,1,0:T(1,128)S(1)}, u32[]{:S(2)}, u32[]{:S(2)}) async-start(f32[4,1,5120]{2,1,0:T(1,128)} %reshape.304), calls=%async_computation.8 | async-start | bytes 163840 | tf_op jit(solution)/shard_map/all_to_all | solution.py:27
  2929.2 52.1 %copy-start.11 = (f32[4,1,5120]{2,1,0:T(1,128)}, f32[4,1,5120]{2,1,0:T(1,128)S(1)}, u32[]{:S(2)}) copy-start(f32[4,1,5120]{2,1,0:T(1,128)S(1)} %all-to-all-done.8) | copy-start | bytes 245764
  2929.2 76.8 %all-to-all-start.9 = ((f32[4,1,5120]{2,1,0:T(1,128)}), f32[4,1,5120]{2,1,0:T(1,128)S(1)}, u32[]{:S(2)}, u32[]{:S(2)}) async-start(f32[4,1,5120]{2,1,0:T(1,128)} %reshape.302), calls=%async_computation.9 | async-start | bytes 163840 | tf_op jit(solution)/shard_map/all_to_all | solution.py:27
  3006.1 405.0 %all-to-all-start.7 = ((bf16[1,64,320,896]{3,1,0,2:T(8,128)(2,1)}), bf16[1,64,320,896]{3,1,0,2:T(8,128)(2,1)}, u32[]{:S(2)}, u32[]{:S(2)}) async-start(bf16[1,64,320,896]{3,1,0,2:T(8,128)(2,1)} %copy.128), calls=%async_computation.7 | async-start | bytes 73400320 | tf_op jit(solution)/shard_map/all_to_all | solution.py:27
  3127.6 295.7 %copy-start.14 = (s32[16384,1]{0,1:T(1,128)S(1)}, s32[16384,1]{0,1:T(1,128)}, u32[]{:S(2)}) copy-start(s32[16384,1]{0,1:T(1,128)} %copy-done.13) | copy-start | bytes 196612
  3127.6 295.8 %copy-start.16 = (s32[16384,1]{0,1:T(1,128)S(1)}, s32[16384,1]{0,1:T(1,128)}, u32[]{:S(2)}) copy-start(s32[16384,1]{0,1:T(1,128)} %copy-done.15) | copy-start | bytes 196612
  3127.6 295.8 %copy-start.12 = (f32[4,1,5120]{2,1,0:T(1,128)S(1)}, f32[4,1,5120]{2,1,0:T(1,128)}, u32[]{:S(2)}) copy-start(f32[4,1,5120]{2,1,0:T(1,128)} %copy-done.11) | copy-start | bytes 245764
  3411.1 854.4 %all-to-all-start.3 = ((bf16[1,64,320,896]{3,1,0,2:T(8,128)(2,1)}), bf16[1,64,320,896]{3,1,0,2:T(8,128)(2,1)}, u32[]{:S(2)}, u32[]{:S(2)}) async-start(bf16[1,64,320,896]{3,1,0,2:T(8,128)(2,1)} %copy.115), calls=%async_computation.3 | async-start | bytes 73400320 | tf_op jit(solution)/shard_map/all_to_all | solution.py:27
  (9 other events, 149.1 us)
Sparse Core Ops, SparseCore 0:
  991.6 339.2 all-gather.7
  1398.3 339.2 all-gather.3
  1805.0 339.2 all-gather.5
  2628.3 636.3 reduce-scatter.5
  3267.3 636.1 reduce-scatter.3
  3906.2 636.1 reduce-scatter.7
where the time goes:
time: 5090 us; the launch traced here: 5060 us
  local copies, waits for them, and re-layouts  2500 us (49%)
  waiting for transfers between devices  1420 us (28%)
  matrix products  772 us (15%)
  other arithmetic  272 us (5%)
  starting transfers between devices  85.7 us (2%)
    gather x2, local copies, waits for them, and re-layouts, local_step(): picked = dx_back[choice_slot].reshape(tok_rows, top_k, d_model)  1190 us
    all_to_all x6, waiting for transfers between devices, to_experts(): arrived = lax.all_to_all(send_buf, 'ep', 0, 2, tiled=True)  1130 us
    all_to_all x4, waiting for transfers between devices, from_experts(): arrived = lax.all_to_all(row_block[None], 'ep', 2, 0, tiled=True)  283 us
    gather x2, local copies, waits for them, and re-layouts, local_step(): jnp.concatenate([gate_prob[mb_index].reshape(n_choice), zero_val])[holder]  226 us
    gather x2, local copies, waits for them, and re-layouts, local_step(): x_send = jnp.concatenate([x_in[mb_index], zero_row], axis=0)[tok_slot]  194 us
    gather x2, local copies, waits for them, and re-layouts, local_step(): dy_send = jnp.concatenate([dy_out[mb_index], zero_row], axis=0)[tok_slot]  194 us
    gather x2, local copies, waits for them, and re-layouts, local_step(): dg_parts.append(dg_back[choice_slot].reshape(tok_rows, top_k))  181 us
    reduce_sum x2, other arithmetic, local_step(): jnp.sum(picked.astype(jnp.float32), axis=1).astype(jnp.bfloat16)  130 us
  transfers between devices with their start and end apart: 16, of which 5 were waited for; matrix products, arithmetic and copies ran while one was open for 60% of the time, Pallas kernels for 0%

commit v1 on v0

v1 whole, which is shorter than its diff:
```python
import functools

import jax
import jax.numpy as jnp
from jax import lax
from jax.experimental import pallas as pl
from jax.experimental.pallas import tpu as pltpu
from jax.sharding import PartitionSpec as P


BF = jnp.bfloat16
F32 = jnp.float32
NT = (((1,), (1,)), ((), ()))
TN = (((0,), (0,)), ((), ()))
LANES = 128
GROUP = 8
CHUNKS = (16, 16, 16, 8, 8)
VMEM_LIMIT = 62 * 2**20


def capacity_of(tok_rows, top_k, experts):
    return 8 * ((5 * tok_rows * top_k + 32 * experts - 1) // (32 * experts))


def params():
    return pltpu.CompilerParams(vmem_limit_bytes=VMEM_LIMIT)


def cost(flops, nbytes):
    return pl.CostEstimate(flops=int(flops), bytes_accessed=int(nbytes), transcendentals=0)


def route_kernel(base_ref, info_ref, pos_ref, gate_ref, choice_ref, *, top_k, capacity):
    experts, tokens = pos_ref.shape[1:]
    ids = (lax.broadcasted_iota(jnp.int32, (experts, tokens), 0) + base_ref[0]).astype(F32)
    member = jnp.zeros((experts, tokens), F32)
    gate = jnp.zeros((experts, tokens), F32)
    choice = jnp.zeros((experts, tokens), F32)
    for j in range(top_k):
        hit = ids == info_ref[0, j:j + 1, :]
        member = jnp.where(hit, 1.0, member)
        gate = jnp.where(hit, info_ref[0, top_k + j:top_k + j + 1, :], gate)
        choice = jnp.where(hit, float(j), choice)
    gate_ref[0] = gate
    choice_ref[0] = choice
    step = 256
    earlier = (lax.broadcasted_iota(jnp.int32, (step, step), 0) < lax.broadcasted_iota(jnp.int32, (step, step), 1))
    earlier = jnp.where(earlier, 1.0, 0.0).astype(BF)
    carry = jnp.zeros((experts, 1), F32)
    for t in range(0, tokens, step):
        block = member[:, t:t + step]
        position = carry + jnp.dot(block.astype(BF), earlier, preferred_element_type=F32)
        kept = jnp.logical_and(block > 0.5, position < capacity)
        pos_ref[0, :, t:t + step] = jnp.where(kept, position, -1.0).astype(BF)
        carry = carry + jnp.sum(block, axis=1, keepdims=True)


def route(base, info, experts, top_k, capacity):
    units, rows, tokens = info.shape
    out = pl.BlockSpec((1, experts, tokens), lambda u: (u, 0, 0))
    shape = (units, experts, tokens)
    return pl.pallas_call(
        functools.partial(route_kernel, top_k=top_k, capacity=capacity),
        grid=(units,),
        in_specs=[pl.BlockSpec(memory_space=pltpu.SMEM), pl.BlockSpec((1, rows, tokens), lambda u: (u, 0, 0))],
        out_specs=[out, out, out],
        out_shape=[jax.ShapeDtypeStruct(shape, BF), jax.ShapeDtypeStruct(shape, F32), jax.ShapeDtypeStruct(shape, F32)],
        compiler_params=params(),
        cost_estimate=cost(units * 1e9, units * experts * tokens * 10),
        name="route",
    )(base, info)


def gather_kernel(*refs, units, aliased):
    pos_ref, gate_ref, choice_ref = refs[:3]
    blocks = refs[3:3 + units]
    refs = refs[3 + units + (2 if aliased else 0):]
    rows_ref, meta_ref, held, sems = refs
    group, _, capacity, width = rows_ref.shape
    tokens = pos_ref.shape[2]
    u, g = pl.program_id(0), pl.program_id(1)

    def fetch(i):
        return pltpu.make_async_copy(blocks[i], held.at[i % 2], sems.at[i % 2])

    for i in range(units):
        @pl.when(jnp.logical_and(u == i, g == 0))
        def _(i=i):
            if i == 0:
                fetch(0).start()
            if i + 1 < units:
                fetch(i + 1).start()
            fetch(i).wait()

    slot = lax.broadcasted_iota(jnp.int32, (capacity, tokens), 0).astype(F32)
    slot_bf = slot.astype(BF)
    lane = lax.broadcasted_iota(jnp.int32, (capacity, LANES), 1)
    picks = []
    for e in range(group):
        row = pos_ref[0, e:e + 1, :]
        picks.append(jnp.where(jnp.broadcast_to(row, (capacity, tokens)) == slot_bf, jnp.ones((), BF), jnp.zeros((), BF)))
        hit = jnp.broadcast_to(row.astype(F32), (capacity, tokens)) == slot
        gate = jnp.sum(jnp.where(hit, gate_ref[0, e:e + 1, :], 0.0), axis=1, keepdims=True)
        choice = jnp.sum(jnp.where(hit, choice_ref[0, e:e + 1, :], 0.0), axis=1, keepdims=True)
        meta_ref[e, 0] = jnp.where(lane == 0, gate, choice)
    one_hot = jnp.concatenate(picks, axis=0)
    rows = jnp.dot(one_hot, held[u % 2], preferred_element_type=F32).astype(BF)
    rows_ref[...] = rows.reshape(group, 1, capacity, width)


def gather(tables, start, blocks, place, total, capacity, buffers):
    pos, gate, choice = tables
    experts, tokens = pos.shape[1:]
    width = blocks[0].shape[1]
    first, stride = place
    units = len(blocks)
    offset, skip = start
    table = pl.BlockSpec((1, GROUP, tokens), lambda u, g: (offset + skip * u, g, 0))
    anywhere = pl.BlockSpec(memory_space=pl.ANY)
    out_map = lambda u, g: (g, first + stride * u, 0, 0)
    aliased = buffers is not None
    n_in = 3 + units
    return pl.pallas_call(
        functools.partial(gather_kernel, units=units, aliased=aliased),
        grid=(units, experts // GROUP),
        in_specs=[table] * 3 + [anywhere] * (units + (2 if aliased else 0)),
        out_specs=[pl.BlockSpec((GROUP, 1, capacity, width), out_map), pl.BlockSpec((GROUP, 1, capacity, LANES), out_map)],
        out_shape=[
            jax.ShapeDtypeStruct((experts, total, capacity, width), BF),
            jax.ShapeDtypeStruct((experts, total, capacity, LANES), F32),
        ],
        scratch_shapes=[pltpu.VMEM((2, tokens, width), BF), pltpu.SemaphoreType.DMA((2,))],
        input_output_aliases={n_in: 0, n_in + 1: 1} if aliased else {},
        compiler_params=params(),
        cost_estimate=cost(2 * units * experts * capacity * tokens * width, units * experts * capacity * width * 4),
        name="gather",
    )(pos, gate, choice, *blocks, *(buffers if aliased else ()))


def expert_kernel(*refs, aliased, own, mine):
    (half_ref, rows_ref, meta_ref, w1, w3, w2, w_got) = refs[:7]
    refs = refs[7 + (3 if aliased else 0):]
    (dw1, dw3, dw2, dx_mine, dx_peer, dg_mine, dg_peer, w_all, g_s, a_s, dh_s, acc_s) = refs
    _, units, capacity, width = rows_ref.shape
    d = width // 2
    half, ff = w1.shape[1:]
    total = units * capacity
    f = half_ref[0]
    near = pl.ds(pl.multiple_of(f * half, half), half)
    far = pl.ds(pl.multiple_of((1 - f) * half, half), half)
    w_all[far, :] = w_got[0]
    w_all[near, 0:ff] = w1[0]
    w_all[near, ff:2 * ff] = w3[0]
    w_all[near, 2 * ff:3 * ff] = w2[0]

    block = 4
    n = block * capacity
    for b in range(0, units, block):
        rows = pl.ds(b * capacity, n)
        x = rows_ref[0, b:b + block, :, 0:d].reshape(n, d)
        dy = rows_ref[0, b:b + block, :, d:2 * d].reshape(n, d)
        meta = meta_ref[0, b:b + block].reshape(n, LANES)
        h = jnp.dot(x, w_all[:, 0:2 * ff], preferred_element_type=F32)
        h1, h3 = h[:, :ff], h[:, ff:]
        sig = jax.nn.sigmoid(h1)
        s = h1 * sig
        a = (s * h3).astype(BF)
        g = (meta[:, 0:1] * dy.astype(F32)).astype(BF)
        da = jnp.dot(g, w_all[:, 2 * ff:3 * ff], preferred_element_type=F32)
        dh3 = (da * s).astype(BF)
        dh1 = (da * h3 * sig * (1.0 + h1 * (1.0 - sig))).astype(BF)
        a_s[rows, :] = a
        g_s[rows, :] = g
        dh_s[rows, 0:ff] = dh1
        dh_s[rows, ff:2 * ff] = dh3
        if b < own:
            dy_w2 = jnp.dot(dy, w_all[:, 2 * ff:3 * ff], preferred_element_type=F32)
            dg = jnp.sum(a.astype(F32) * dy_w2, axis=1, keepdims=True)
            lane = lax.broadcasted_iota(jnp.int32, (n, LANES), 1).astype(F32)
            dg = jnp.where(lane == meta[:, 1:2], dg, 0.0)
            dh = jnp.concatenate([dh1, dh3], axis=1)
            dx = lax.dot_general(dh, w_all[:, 0:2 * ff], NT, preferred_element_type=F32)
            to_x, to_g, at = (dx_mine, dg_mine, b) if b < mine else (dx_peer, dg_peer, b - mine)
            to_x[0, at:at + block] = dx.astype(BF).reshape(block, capacity, d)
            to_g[0, at:at + block] = dg.reshape(block, capacity, LANES)

    window = acc_s.shape[0]
    lo = pl.multiple_of(f * (d - window), LANES)
    keep = pl.ds(pl.multiple_of(f * (window - half), window - half), half)
    x_win = rows_ref[0, :, :, pl.ds(lo, window)].reshape(total, window)
    acc_s[:, 0:2 * ff] = lax.dot_general(x_win, dh_s[...], TN, preferred_element_type=F32)
    acc_s[:, 2 * ff:3 * ff] = lax.dot_general(g_s[:, pl.ds(lo, window)], a_s[...], TN, preferred_element_type=F32)
    dw1[0] = acc_s[keep, 0:ff]
    dw3[0] = acc_s[keep, ff:2 * ff]
    dw2[0] = acc_s[keep, 2 * ff:3 * ff]


def experts_pass(half, rows, meta, weights, w_got, first, grads, own, mine):
    n = w_got.shape[0]
    experts, units, capacity, width = rows.shape
    d = width // 2
    dh, ff = weights[0].shape[1:]
    at = lambda *s: pl.BlockSpec((1,) + s, lambda e: (e + first,) + (0,) * len(s))
    loc = lambda *s: pl.BlockSpec((1,) + s, lambda e: (e,) + (0,) * len(s))
    anywhere = pl.BlockSpec(memory_space=pl.ANY)
    aliased = grads is not None
    total = units * capacity
    window = -(-dh // LANES) * LANES
    grad = jax.ShapeDtypeStruct((experts, dh, ff), F32)
    flops = n * 2 * total * d * ff * 6
    return pl.pallas_call(
        functools.partial(expert_kernel, aliased=aliased, own=own, mine=mine),
        grid=(n,),
        in_specs=[pl.BlockSpec(memory_space=pltpu.SMEM), at(units, capacity, width), at(units, capacity, LANES)]
        + [at(dh, ff)] * 3 + [loc(dh, 3 * ff)] + [anywhere] * (3 if aliased else 0),
        out_specs=[at(dh, ff)] * 3 + [loc(mine, capacity, d), loc(own - mine, capacity, d),
                                      loc(mine, capacity, LANES), loc(own - mine, capacity, LANES)],
        out_shape=[
            grad,
            grad,
            grad,
            jax.ShapeDtypeStruct((n, mine, capacity, d), BF),
            jax.ShapeDtypeStruct((n, own - mine, capacity, d), BF),
            jax.ShapeDtypeStruct((n, mine, capacity, LANES), F32),
            jax.ShapeDtypeStruct((n, own - mine, capacity, LANES), F32),
        ],
        scratch_shapes=[
            pltpu.VMEM((d, 3 * ff), BF),
            pltpu.VMEM((total, d), BF),
            pltpu.VMEM((total, ff), BF),
            pltpu.VMEM((total, 2 * ff), BF),
            pltpu.VMEM((window, 3 * ff), F32),
        ],
        input_output_aliases={7: 0, 8: 1, 9: 2} if aliased else {},
        compiler_params=params(),
        cost_estimate=cost(flops, n * total * width * 2),
        name="experts",
    )(half, rows, meta, *weights, w_got, *(grads if aliased else ()))


def combine_kernel(*refs, top_k, has_prev, last):
    pos_own, pos_peer, dx_own, dx_peer, dg_own, dg_peer = refs[:6]
    prev = refs[6] if has_prev else None
    refs = refs[6 + (1 if has_prev else 0):]
    if last:
        sum_ref, gate_ref, acc, rhs = refs
    else:
        acc, rhs = refs
        acc = acc.at[0]
    group, _, capacity, d = dx_own.shape
    tokens = pos_own.shape[2]
    g = pl.program_id(1)

    @pl.when(g == 0)
    def _():
        if has_prev:
            acc[...] = prev[0]
        else:
            acc[...] = jnp.zeros(acc.shape, F32)

    n = group * capacity
    for i, (dx, dg) in enumerate(((dx_own, dg_own), (dx_peer, dg_peer))):
        rhs[i * n:(i + 1) * n, 0:d] = dx[...].reshape(n, d)
        val = dg[...].reshape(n, LANES)
        high = val.astype(BF).astype(F32)
        mid = (val - high).astype(BF).astype(F32)
        low = val - high - mid
        packed = high + pltpu.roll(mid, top_k, 1) + pltpu.roll(low, 2 * top_k, 1)
        rhs[i * n:(i + 1) * n, d:d + LANES] = packed.astype(BF)
    slot = lax.broadcasted_iota(jnp.int32, (capacity, tokens), 0).astype(F32).astype(BF)
    picks = []
    for pos in (pos_own, pos_peer):
        for e in range(group):
            row = jnp.broadcast_to(pos[0, e:e + 1, :], (capacity, tokens))
            picks.append(jnp.where(row == slot, jnp.ones((), BF), jnp.zeros((), BF)))
    one_hot = jnp.concatenate(picks, axis=0)
    acc[...] += lax.dot_general(one_hot, rhs[...], TN, preferred_element_type=F32)
    if last:
        @pl.when(g == pl.num_programs(1) - 1)
        def _():
            sum_ref[0] = acc[:, 0:d]
            part = acc[:, d:d + LANES]
            part = part + pltpu.roll(part, LANES - top_k, 1) + pltpu.roll(part, LANES - 2 * top_k, 1)
            gate_ref[0] = part.T[0:top_k, :]


def combine(pos_own, pos_peer, pieces, prev, first, unit0, units, top_k, last):
    dx_own, dx_peer, dg_own, dg_peer = pieces
    n, _, capacity, d = dx_own.shape
    tokens = pos_own.shape[2]
    group = 4 if n % GROUP else GROUP
    assert first % group == 0
    base = first // group
    table = pl.BlockSpec((1, group, tokens), lambda u, g: (u + unit0, g + base, 0))
    rows = lambda w: pl.BlockSpec((group, 1, capacity, w), lambda u, g: (g, u + unit0, 0, 0))
    whole = lambda shift, *s: pl.BlockSpec((1,) + s, lambda u, g: (u + shift,) + (0,) * len(s))
    has_prev = prev is not None
    wide = d + LANES
    if last:
        out_specs = [whole(0, tokens, d), whole(0, top_k, tokens)]
        out_shape = [jax.ShapeDtypeStruct((units, tokens, d), F32), jax.ShapeDtypeStruct((units, top_k, tokens), F32)]
        scratch = [pltpu.VMEM((tokens, wide), F32)]
    else:
        out_specs = whole(0, tokens, wide)
        out_shape = jax.ShapeDtypeStruct((units, tokens, wide), F32)
        scratch = []
    scratch = scratch + [pltpu.VMEM((2 * group * capacity, wide), BF)]
    return pl.pallas_call(
        functools.partial(combine_kernel, top_k=top_k, has_prev=has_prev, last=last),
        grid=(units, n // group),
        in_specs=[table, table, rows(d), rows(d), rows(LANES), rows(LANES)]
        + ([pl.BlockSpec((1, tokens, wide), lambda u, g: (u + unit0, 0, 0))] if has_prev else []),
        out_specs=out_specs,
        out_shape=out_shape,
        scratch_shapes=scratch,
        compiler_params=params(),
        cost_estimate=cost(4 * units * n * capacity * tokens * wide, units * tokens * wide * 8),
        name="combine",
    )(pos_own, pos_peer, dx_own, dx_peer, dg_own, dg_peer, *((prev,) if has_prev else ()))


def solution(mesh):
    tok_spec = P(None, ('fsdp', 'ep'), None)
    spec_edf = P('ep', 'fsdp', None)
    spec_efd = P('ep', None, 'fsdp')

    def over_y(v):
        return lax.ppermute(v, 'fsdp', [(0, 1), (1, 0)])

    def over_x(v):
        return lax.ppermute(v, 'ep', [(0, 2), (1, 3), (2, 0), (3, 1)])

    def over_core(v):
        return lax.ppermute(v, 'ep', [(0, 1), (1, 0), (2, 3), (3, 2)])

    def step(x_in, dy_out, expert_idx, gate_prob, w_one, w_two, w_three):
        micro, tokens, _ = x_in.shape
        top_k = expert_idx.shape[2]
        local = w_one.shape[0]
        capacity = capacity_of(tokens, top_k, local * 4)
        f, ep = lax.axis_index('fsdp'), lax.axis_index('ep')
        half = f.astype(jnp.int32).reshape(1)
        base_own = (ep * local).astype(jnp.int32).reshape(1)
        base_peer = ((ep ^ 1) * local).astype(jnp.int32).reshape(1)

        def tables(info, base=base_own):
            return route(base, info, local, top_k, capacity)

        info = jnp.concatenate([jnp.swapaxes(expert_idx, 1, 2).astype(F32), jnp.swapaxes(gate_prob, 1, 2)], axis=1)
        b = [jnp.concatenate([x_in[m], dy_out[m]], axis=1) for m in range(micro)]
        iy = over_y(info)
        ix = over_x(info)
        ic = over_core(info)
        near = jnp.concatenate([iy, ix])
        near_c = over_core(near)
        idg = over_x(iy)
        idc = over_core(idg)
        t_own = tables(info)
        t_core = tables(ic)
        t_near = tables(jnp.concatenate([near, near_c]))
        t_diag = tables(jnp.concatenate([idg, idc]))
        pos_own = jnp.concatenate([t_own[0], t_near[0][2:4]])
        pos_peer = tables(jnp.concatenate([info, ix]), base_peer)[0]

        w_two_t = jnp.swapaxes(w_two, 1, 2)
        weights = (w_one, w_three, w_two_t)
        y = [over_y(b[m]) for m in range(micro)]
        x = [over_x(b[m]) for m in range(micro)]
        d = [over_x(y[m]) for m in range(micro)]
        bc, yc, xc, dc = ([over_core(v[m]) for m in range(micro)] for v in (b, y, x, d))
        got = []
        first = 0
        for n in CHUNKS:
            got.append(over_y(jnp.concatenate([w[first:first + n] for w in weights], axis=2)))
            first += n

        calls = [
            (t_own, (0, 1), b, (0, 1)),
            (t_core, (0, 1), bc, (4, 1)),
            (t_near, (0, 2), [y[0], x[0]], (8, -6)),
            (t_near, (4, 2), [yc[0], xc[0]], (12, -6)),
            (t_near, (1, 2), [y[1], x[1]], (9, -6)),
            (t_near, (5, 2), [yc[1], xc[1]], (13, -6)),
            (t_diag, (0, 2), [d[0], dc[0]], (10, 4)),
            (t_diag, (1, 2), [d[1]], (11, 4)),
            (t_diag, (3, 2), [dc[1]], (15, 4)),
        ]
        buffers = None
        for table, start, blocks, place in calls:
            buffers = gather(table, start, blocks, place, 16, capacity, buffers)
        rows, meta = buffers

        grads = None
        partial = None
        first = 0
        for k, n in enumerate(CHUNKS):
            res = experts_pass(half, rows, meta, weights, got[k], first, grads, 8, 4)
            grads = res[:3]
            pieces = (res[3], over_core(res[4]), res[5], over_core(res[6]))

            def combined(*rest):
                return combine(pos_own, pos_peer, pieces, partial, first, *rest)

            if k + 1 < len(CHUNKS):
                partial = combined(0, 4, top_k, False)
            else:
                away = [combined(2 + m, 1, top_k, True) for m in range(micro)]
                back = [(over_x(away[m][0]), over_x(away[m][1])) for m in range(micro)]
                home = [combined(m, 1, top_k, True) for m in range(micro)]
            first += n
        dx = [(h[0][0] + r[0][0]).astype(BF) for h, r in zip(home, back)]
        dg = [(h[1][0] + r[1][0]).T for h, r in zip(home, back)]
        return jnp.stack(dx), jnp.stack(dg), grads[0], jnp.swapaxes(grads[2], 1, 2), grads[1]

    return jax.shard_map(step, mesh=mesh, in_specs=(tok_spec, tok_spec, tok_spec, tok_spec, spec_edf, spec_efd, spec_edf), out_specs=(tok_spec, tok_spec, spec_edf, spec_efd, spec_edf), check_vma=False)
```

time: 5090 us -> 2060 us (0.40)
  local copies, waits for them, and re-layouts: 2500 us -> 39.4 us
  Pallas kernels: 0 us -> 1410 us
  waiting for transfers between devices: 1420 us -> 523 us
  matrix products: 772 us -> 0 us
  other arithmetic: 272 us -> 54.2 us
  starting transfers between devices: 85.7 us -> 20.1 us
    gather x10 -> x0, local copies, waits for them, and re-layouts: 1990 us -> none  [the longest x2 1190 us: local_step(): picked = dx_back[choice_slot].reshape(tok_rows, top_k, d_model)]
    all_to_all x10 -> x0, waiting for transfers between devices: 1410 us -> none  [the longest x6 1130 us: to_experts(): arrived = lax.all_to_all(send_buf, 'ep', 0, 2, tiled=True)]
    pallas_call x0 -> x27, Pallas kernels: none -> 1410 us  [the longest x9 784 us: gather(): pl.pallas_call(functools.partial(gather_kernel, units=units, aliased=alia...]
    dot_general x18 -> x0, matrix products: 772 us -> none  [the longest x2 111 us: expert_pass(): jnp.einsum('erf,erd->efd', act_bf, g_rows, preferred_element_type=jnp.flo...]
    ppermute x0 -> x39, waiting for transfers between devices: none -> 523 us  [the longest x10 403 us: over_x(): return lax.ppermute(v, 'ep', [(0, 2), (1, 3), (2, 0), (3, 1)])]
    reduce_sum x4 -> x0, other arithmetic: 145 us -> none  [the longest x2 130 us: local_step(): jnp.sum(picked.astype(jnp.float32), axis=1).astype(jnp.bfloat16)]
    scatter x2 -> x0, local copies, waits for them, and re-layouts: 121 us -> none  [route_tables(): holder = holder.at[choice_slot].set(jnp.arange(n_choice, dtype=jnp.int32))]
    all_to_all x10 -> x0, local copies, waits for them, and re-layouts: 117 us -> none  [the longest x6 66.6 us: from_experts(): arrived = lax.all_to_all(row_block[None], 'ep', 2, 0, tiled=True)]
  transfers between devices with their start and end apart: 16 -> 39, of which waited for: 5 -> 9; matrix products, arithmetic and copies ran while one was open for 60% -> 3% of each run, Pallas kernels for 0% -> 68%
where the time goes in v1:
time: 2060 us; the launch traced here: 2050 us
  Pallas kernels  1410 us (68%)
  waiting for transfers between devices  523 us (25%)
  other arithmetic  54.2 us (3%)
  local copies, waits for them, and re-layouts  39.4 us (2%)
    pallas_call x9, Pallas kernels, gather(): pl.pallas_call(functools.partial(gather_kernel, units=units, aliased=alia...  784 us
    ppermute x10, waiting for transfers between devices, over_x(): return lax.ppermute(v, 'ep', [(0, 2), (1, 3), (2, 0), (3, 1)])  403 us
    pallas_call x5, Pallas kernels, experts_pass(): pl.pallas_call(functools.partial(expert_kernel, aliased=aliased, own=own,...  348 us
    pallas_call x8, Pallas kernels, combine(): pl.pallas_call(functools.partial(combine_kernel, top_k=top_k, has_prev=ha...  253 us
    ppermute x8, waiting for transfers between devices, over_y(): return lax.ppermute(v, 'fsdp', [(0, 1), (1, 0)])  120 us
  transfers between devices with their start and end apart: 39, of which 9 were waited for; matrix products, arithmetic and copies ran while one was open for 3% of the time, Pallas kernels for 68%

profile of v1, /device:TPU:6, one launch (start us, length us, event | category | flops | bytes accessed | tf_op | source)
XLA Modules:
  0.0 2050.9 jit_solution(6751412244393435015)
XLA Ops:
  27.3 97.2 %gather.9 = (bf16[64,16,80,1792]{3,2,1,0:T(8,128)(2,1)}, f32[64,16,80,128]{3,2,1,0:T(8,128)}) custom-call(bf16[2,64,2048]{2,1,0:T(8,128)(2,1)} %get-tuple-element.79.refs_0_, f32[2,64,2048]{2,1,0:T(8,128)} %get-tuple-element.90.refs_1_, f32[2,64,2048]{2,1,0:T(8,128)} %get-tuple-element.91.refs_2_, bf16[2048,1792]{1,0:T(8,128)(2,1)} %pad_maximum_fusion.4.refs_3_, ...), custom_call_target="tpu_custom_call" | custom-call | flops 75161927680 | bytes 73400320 | tf_op jit(solution)/shard_map/gather/pallas_call | solution.py:123
  169.2 14.2 collective-permute-done
  229.0 97.2 %gather.10 = (bf16[64,16,80,1792]{3,2,1,0:T(8,128)(2,1)}, f32[64,16,80,128]{3,2,1,0:T(8,128)}) custom-call(bf16[2,64,2048]{2,1,0:T(8,128)(2,1)} %get-tuple-element.87.refs_0_, f32[2,64,2048]{2,1,0:T(8,128)} %get-tuple-element.88.refs_1_, f32[2,64,2048]{2,1,0:T(8,128)} %get-tuple-element.89.refs_2_, ...), custom_call_target="tpu_custom_call", output_to_operand_aliasing={{0}: (5, {}), {1}: (6, {})} | custom-call | flops 75161927680 | bytes 73400320 | tf_op jit(solution)/shard_map/gather/pallas_call | solution.py:123
  326.2 97.3 %gather.11 = (bf16[64,16,80,1792]{3,2,1,0:T(8,128)(2,1)}, f32[64,16,80,128]{3,2,1,0:T(8,128)}) custom-call(bf16[8,64,2048]{2,1,0:T(8,128)(2,1)} %get-tuple-element.80.refs_0_, f32[8,64,2048]{2,1,0:T(8,128)} %get-tuple-element.85.refs_1_, f32[8,64,2048]{2,1,0:T(8,128)} %get-tuple-element.86.refs_2_, ...), custom_call_target="tpu_custom_call", output_to_operand_aliasing={{0}: (5, {}), {1}: (6, {})} | custom-call | flops 75161927680 | bytes 73400320 | tf_op jit(solution)/shard_map/gather/pallas_call | solution.py:123
  425.9 119.3 %collective-permute-done.9.refs_3_ = bf16[2048,1792]{1,0:T(8,128)(2,1)} collective-permute-done((bf16[2048,1792]{1,0:T(8,128)(2,1)}, bf16[2048,1792]{1,0:T(8,128)(2,1)}, u32[]{:S(2)}, u32[]{:S(2)}) %collective-permute-start.9) | collective-permute-done | bytes 7340064 | tf_op jit(solution)/shard_map/ppermute | solution.py:331
  545.2 97.7 %gather.12 = (bf16[64,16,80,1792]{3,2,1,0:T(8,128)(2,1)}, f32[64,16,80,128]{3,2,1,0:T(8,128)}) custom-call(bf16[8,64,2048]{2,1,0:T(8,128)(2,1)} %get-tuple-element.80.refs_0_, f32[8,64,2048]{2,1,0:T(8,128)} %get-tuple-element.85.refs_1_, f32[8,64,2048]{2,1,0:T(8,128)} %get-tuple-element.86.refs_2_, ...), custom_call_target="tpu_custom_call", output_to_operand_aliasing={{0}: (5, {}), {1}: (6, {})} | custom-call | flops 75161927680 | bytes 73400320 | tf_op jit(solution)/shard_map/gather/pallas_call | solution.py:123
  642.9 97.3 %gather.13 = (bf16[64,16,80,1792]{3,2,1,0:T(8,128)(2,1)}, f32[64,16,80,128]{3,2,1,0:T(8,128)}) custom-call(bf16[8,64,2048]{2,1,0:T(8,128)(2,1)} %get-tuple-element.80.refs_0_, f32[8,64,2048]{2,1,0:T(8,128)} %get-tuple-element.85.refs_1_, f32[8,64,2048]{2,1,0:T(8,128)} %get-tuple-element.86.refs_2_, ...), custom_call_target="tpu_custom_call", output_to_operand_aliasing={{0}: (5, {}), {1}: (6, {})} | custom-call | flops 75161927680 | bytes 73400320 | tf_op jit(solution)/shard_map/gather/pallas_call | solution.py:123
  742.2 97.4 %gather.14 = (bf16[64,16,80,1792]{3,2,1,0:T(8,128)(2,1)}, f32[64,16,80,128]{3,2,1,0:T(8,128)}) custom-call(bf16[8,64,2048]{2,1,0:T(8,128)(2,1)} %get-tuple-element.80.refs_0_, f32[8,64,2048]{2,1,0:T(8,128)} %get-tuple-element.85.refs_1_, f32[8,64,2048]{2,1,0:T(8,128)} %get-tuple-element.86.refs_2_, ...), custom_call_target="tpu_custom_call", output_to_operand_aliasing={{0}: (5, {}), {1}: (6, {})} | custom-call | flops 75161927680 | bytes 73400320 | tf_op jit(solution)/shard_map/gather/pallas_call | solution.py:123
  841.2 97.2 %gather.15 = (bf16[64,16,80,1792]{3,2,1,0:T(8,128)(2,1)}, f32[64,16,80,128]{3,2,1,0:T(8,128)}) custom-call(bf16[4,64,2048]{2,1,0:T(8,128)(2,1)} %get-tuple-element.82.refs_0_, f32[4,64,2048]{2,1,0:T(8,128)} %get-tuple-element.83.refs_1_, f32[4,64,2048]{2,1,0:T(8,128)} %get-tuple-element.84.refs_2_, ...), custom_call_target="tpu_custom_call", output_to_operand_aliasing={{0}: (5, {}), {1}: (6, {})} | custom-call | flops 75161927680 | bytes 73400320 | tf_op jit(solution)/shard_map/gather/pallas_call | solution.py:123
  938.5 51.5 %gather.16 = (bf16[64,16,80,1792]{3,2,1,0:T(8,128)(2,1)}, f32[64,16,80,128]{3,2,1,0:T(8,128)}) custom-call(bf16[4,64,2048]{2,1,0:T(8,128)(2,1)} %get-tuple-element.82.refs_0_, f32[4,64,2048]{2,1,0:T(8,128)} %get-tuple-element.83.refs_1_, f32[4,64,2048]{2,1,0:T(8,128)} %get-tuple-element.84.refs_2_, ...), custom_call_target="tpu_custom_call", output_to_operand_aliasing={{0}: (4, {}), {1}: (5, {})} | custom-call | flops 37580963840 | bytes 36700160 | tf_op jit(solution)/shard_map/gather/pallas_call | solution.py:123
  990.5 51.2 %gather.17 = (bf16[64,16,80,1792]{3,2,1,0:T(8,128)(2,1)}, f32[64,16,80,128]{3,2,1,0:T(8,128)}) custom-call(bf16[4,64,2048]{2,1,0:T(8,128)(2,1)} %get-tuple-element.82.refs_0_, f32[4,64,2048]{2,1,0:T(8,128)} %get-tuple-element.83.refs_1_, f32[4,64,2048]{2,1,0:T(8,128)} %get-tuple-element.84.refs_2_, ...), custom_call_target="tpu_custom_call", output_to_operand_aliasing={{0}: (4, {}), {1}: (5, {})} | custom-call | flops 37580963840 | bytes 36700160 | tf_op jit(solution)/shard_map/gather/pallas_call | solution.py:123
  1041.8 86.2 %experts.5 = (f32[64,448,256]{2,1,0:T(8,128)}, f32[64,448,256]{2,1,0:T(8,128)}, f32[64,448,256]{2,1,0:T(8,128)}, bf16[16,4,80,896]{3,2,1,0:T(8,128)(2,1)}, bf16[...) custom-call(s32[1]{0:T(128)} %bitcast.4.refs_0_, ...), custom_call_target="tpu_custom_call" | custom-call | flops 56371445760 | bytes 73400320 | tf_op jit(solution)/shard_map/experts/pallas_call | solution.py:211
  1128.5 85.9 %experts.6 = (f32[64,448,256]{2,1,0:T(8,128)}, f32[64,448,256]{2,1,0:T(8,128)}, f32[64,448,256]{2,1,0:T(8,128)}, bf16[16,4,80,896]{3,2,1,0:T(8,128)(2,1)}, bf16[...) custom-call(s32[1]{0:T(128)} %bitcast.4.refs_0_, ...), custom_call_target="tpu_custom_call", output_to_operand_aliasing={{0}: (7, {}), {1}: (8, {}), {2}: (9, {})} | custom-call | flops 56371445760 | bytes 73400320 | tf_op jit(solution)/shard_map/experts/pallas_call | solution.py:211
  1216.0 86.4 %experts.7 = (f32[64,448,256]{2,1,0:T(8,128)}, f32[64,448,256]{2,1,0:T(8,128)}, f32[64,448,256]{2,1,0:T(8,128)}, bf16[16,4,80,896]{3,2,1,0:T(8,128)(2,1)}, bf16[...) custom-call(s32[1]{0:T(128)} %bitcast.4.refs_0_, ...), custom_call_target="tpu_custom_call", output_to_operand_aliasing={{0}: (7, {}), {1}: (8, {}), {2}: (9, {})} | custom-call | flops 56371445760 | bytes 73400320 | tf_op jit(solution)/shard_map/experts/pallas_call | solution.py:211
  1302.3 31.6 %collective-permute-done.21.refs_6_ = bf16[8,448,768]{2,1,0:T(8,128)(2,1)} collective-permute-done((bf16[8,448,768]{2,1,0:T(8,128)(2,1)}, bf16[8,448,768]{2,1,0:T(8,128)(2,1)}, u32[]{:S(2)}, u32[]{:S(2)}) %collective-permute-start.21) | collective-permute-done | bytes 5505056 | tf_op jit(solution)/shard_map/ppermute | solution.py:328
  1333.9 44.9 %experts.8 = (f32[64,448,256]{2,1,0:T(8,128)}, f32[64,448,256]{2,1,0:T(8,128)}, f32[64,448,256]{2,1,0:T(8,128)}, bf16[8,4,80,896]{3,2,1,0:T(8,128)(2,1)}, bf16[8...) custom-call(s32[1]{0:T(128)} %bitcast.4.refs_0_, ...), custom_call_target="tpu_custom_call", output_to_operand_aliasing={{0}: (7, {}), {1}: (8, {}), {2}: (9, {})} | custom-call | flops 28185722880 | bytes 36700160 | tf_op jit(solution)/shard_map/experts/pallas_call | solution.py:211
  1378.8 72.6 %collective-permute-done.20.refs_6_ = bf16[8,448,768]{2,1,0:T(8,128)(2,1)} collective-permute-done((bf16[8,448,768]{2,1,0:T(8,128)(2,1)}, bf16[8,448,768]{2,1,0:T(8,128)(2,1)}, u32[]{:S(2)}, u32[]{:S(2)}) %collective-permute-start.20) | collective-permute-done | bytes 5505056 | tf_op jit(solution)/shard_map/ppermute | solution.py:328
  1451.4 45.1 %experts.9 = (f32[64,448,256]{2,1,0:T(8,128)}, f32[64,448,256]{2,1,0:T(8,128)}, f32[64,448,256]{2,1,0:T(8,128)}, bf16[8,4,80,896]{3,2,1,0:T(8,128)(2,1)}, bf16[8...) custom-call(s32[1]{0:T(128)} %bitcast.4.refs_0_, ...), custom_call_target="tpu_custom_call", output_to_operand_aliasing={{0}: (7, {}), {1}: (8, {}), {2}: (9, {})} | custom-call | flops 28185722880 | bytes 36700160 | tf_op jit(solution)/shard_map/experts/pallas_call | solution.py:211
  1497.1 53.7 %combine.8.refs_6_ = f32[4,2048,1024]{2,1,0:T(8,128)} custom-call(bf16[4,64,2048]{2,1,0:T(8,128)(2,1)} %pad_maximum_fusion.9.refs_0_, bf16[4,64,2048]{2,1,0:T(8,128)(2,1)} %get-tuple-element.81.refs_1_, bf16[16,4,80,896]{3,2,1,0:T(8,128)(2,1)} %get-tuple-element.138.refs_2_, bf16[16,4,80,896]{3,2,1,0:T(8,128)(2,1)} %collective-permute-done.33.refs_3_, ...), custom_call_target="tpu_custom_call" | custom-call | flops 42949672960 | bytes 67108864 | tf_op jit(solution)/shard_map/combine/pallas_call | solution.py:308
  1551.4 56.8 %combine.9.refs_6_ = f32[4,2048,1024]{2,1,0:T(8,128)} custom-call(bf16[4,64,2048]{2,1,0:T(8,128)(2,1)} %pad_maximum_fusion.9.refs_0_, bf16[4,64,2048]{2,1,0:T(8,128)(2,1)} %get-tuple-element.81.refs_1_, bf16[16,4,80,896]{3,2,1,0:T(8,128)(2,1)} %get-tuple-element.134.refs_2_, bf16[16,4,80,896]{3,2,1,0:T(8,128)(2,1)} %collective-permute-done.31.refs_3_, ...), custom_call_target="tpu_custom_call" | custom-call | flops 42949672960 | bytes 67108864 | tf_op jit(solution)/shard_map/combine/pallas_call | solution.py:308
  1608.7 56.5 %combine.10.refs_6_ = f32[4,2048,1024]{2,1,0:T(8,128)} custom-call(bf16[4,64,2048]{2,1,0:T(8,128)(2,1)} %pad_maximum_fusion.9.refs_0_, bf16[4,64,2048]{2,1,0:T(8,128)(2,1)} %get-tuple-element.81.refs_1_, bf16[16,4,80,896]{3,2,1,0:T(8,128)(2,1)} %get-tuple-element.130.refs_2_, bf16[16,4,80,896]{3,2,1,0:T(8,128)(2,1)} %collective-permute-done.29.refs_3_, ...), custom_call_target="tpu_custom_call" | custom-call | flops 42949672960 | bytes 67108864 | tf_op jit(solution)/shard_map/combine/pallas_call | solution.py:308
  1665.3 33.7 %combine.11.refs_6_ = f32[4,2048,1024]{2,1,0:T(8,128)} custom-call(bf16[4,64,2048]{2,1,0:T(8,128)(2,1)} %pad_maximum_fusion.9.refs_0_, bf16[4,64,2048]{2,1,0:T(8,128)(2,1)} %get-tuple-element.81.refs_1_, bf16[8,4,80,896]{3,2,1,0:T(8,128)(2,1)} %get-tuple-element.126.refs_2_, bf16[8,4,80,896]{3,2,1,0:T(8,128)(2,1)} %collective-permute-done.27.refs_3_, ...), custom_call_target="tpu_custom_call" | custom-call | flops 21474836480 | bytes 67108864 | tf_op jit(solution)/shard_map/combine/pallas_call | solution.py:308
  1730.3 13.4 combine.12
  1756.8 276.0 %collective-permute-done.37 = f32[1,8,2048]{2,1,0:T(8,128)S(1)} collective-permute-done((f32[1,8,2048]{2,1,0:T(8,128)S(1)}, f32[1,8,2048]{2,1,0:T(8,128)S(1)}, u32[]{:S(2)}, u32[]{:S(2)}) %collective-permute-start.37) | collective-permute-done | bytes 65568 | tf_op jit(solution)/shard_map/ppermute | solution.py:331
  (132 shorter events, 189.1 us)
Async XLA Ops:
  17.2 209.5 %collective-permute-start.18 = (bf16[2048,1792]{1,0:T(8,128)(2,1)}, bf16[2048,1792]{1,0:T(8,128)(2,1)}, u32[]{:S(2)}, u32[]{:S(2)}) collective-permute-start(bf16[2048,1792]{1,0:T(8,128)(2,1)} %pad_maximum_fusion.4.refs_3_), channel_id=1, source_target_pairs={{0,1},{1,0},{2,3},{3,2},{4,5},{5,4},{6,7},{7,6}} | collective-permute-start | bytes 22020104 | tf_op jit(solution)/shard_map/ppermute | solution.py:334
  17.2 210.4 %collective-permute-start.8 = (bf16[2048,1792]{1,0:T(8,128)(2,1)}, bf16[2048,1792]{1,0:T(8,128)(2,1)}, u32[]{:S(2)}, u32[]{:S(2)}) collective-permute-start(bf16[2048,1792]{1,0:T(8,128)(2,1)} %pad_maximum_fusion.4.refs_3_), channel_id=1, source_target_pairs={{0,4},{4,0},{1,5},{5,1},{2,6},{6,2},{3,7},{7,3}} | collective-permute-start | bytes 22020104 | tf_op jit(solution)/shard_map/ppermute | solution.py:328
  17.7 211.1 %collective-permute-start.15 = (bf16[2048,1792]{1,0:T(8,128)(2,1)}, bf16[2048,1792]{1,0:T(8,128)(2,1)}, u32[]{:S(2)}, u32[]{:S(2)}) collective-permute-start(bf16[2048,1792]{1,0:T(8,128)(2,1)} %pad_maximum_fusion.4.refs_3_), channel_id=1, source_target_pairs={{0,2},{1,3},{2,0},{3,1},{4,6},{5,7},{6,4},{7,5}} | collective-permute-start | bytes 22020104 | tf_op jit(solution)/shard_map/ppermute | solution.py:331
  23.7 203.9 %collective-permute-start.19 = (bf16[2048,1792]{1,0:T(8,128)(2,1)}, bf16[2048,1792]{1,0:T(8,128)(2,1)}, u32[]{:S(2)}, u32[]{:S(2)}) collective-permute-start(bf16[2048,1792]{1,0:T(8,128)(2,1)} %pad_maximum_fusion.3.refs_4_), channel_id=1, source_target_pairs={{0,1},{1,0},{2,3},{3,2},{4,5},{5,4},{6,7},{7,6}} | collective-permute-start | bytes 22020104 | tf_op jit(solution)/shard_map/ppermute | solution.py:334
  218.8 204.8 %collective-permute-start.5 = (bf16[2048,1792]{1,0:T(8,128)(2,1)}, bf16[2048,1792]{1,0:T(8,128)(2,1)}, u32[]{:S(2)}, u32[]{:S(2)}) collective-permute-start(bf16[2048,1792]{1,0:T(8,128)(2,1)} %pad_maximum_fusion.3.refs_4_), channel_id=1, source_target_pairs={{0,4},{4,0},{1,5},{5,1},{2,6},{6,2},{3,7},{7,3}} | collective-permute-start | bytes 22020104 | tf_op jit(solution)/shard_map/ppermute | solution.py:328
  226.7 198.4 %collective-permute-start.12 = (bf16[2048,1792]{1,0:T(8,128)(2,1)}, bf16[2048,1792]{1,0:T(8,128)(2,1)}, u32[]{:S(2)}, u32[]{:S(2)}) collective-permute-start(bf16[2048,1792]{1,0:T(8,128)(2,1)} %pad_maximum_fusion.3.refs_4_), channel_id=1, source_target_pairs={{0,2},{1,3},{2,0},{3,1},{4,6},{5,7},{6,4},{7,5}} | collective-permute-start | bytes 22020104 | tf_op jit(solution)/shard_map/ppermute | solution.py:331
  227.6 317.6 %collective-permute-start.9 = (bf16[2048,1792]{1,0:T(8,128)(2,1)}, bf16[2048,1792]{1,0:T(8,128)(2,1)}, u32[]{:S(2)}, u32[]{:S(2)}) collective-permute-start(bf16[2048,1792]{1,0:T(8,128)(2,1)} %collective-permute-done.8.refs_3_), channel_id=1, source_target_pairs={{0,2},{1,3},{2,0},{3,1},{4,6},{5,7},{6,4},{7,5}} | collective-permute-start | bytes 22020104 | tf_op jit(solution)/shard_map/ppermute | solution.py:331
  423.6 618.2 %collective-permute-start.24 = (bf16[16,448,768]{2,1,0:T(8,128)(2,1)}, bf16[16,448,768]{2,1,0:T(8,128)(2,1)}, u32[]{:S(2)}, u32[]{:S(2)}) collective-permute-start(bf16[16,448,768]{2,1,0:T(8,128)(2,1)} %pad_maximum_fusion.2), channel_id=1, source_target_pairs={{0,4},{4,0},{1,5},{5,1},{2,6},{6,2},{3,7},{7,3}} | collective-permute-start | bytes 33030152 | tf_op jit(solution)/shard_map/ppermute | solution.py:328
  425.1 315.1 %collective-permute-start.11 = (bf16[2048,1792]{1,0:T(8,128)(2,1)}, bf16[2048,1792]{1,0:T(8,128)(2,1)}, u32[]{:S(2)}, u32[]{:S(2)}) collective-permute-start(bf16[2048,1792]{1,0:T(8,128)(2,1)} %collective-permute-done.5.refs_3_), channel_id=1, source_target_pairs={{0,1},{1,0},{2,3},{3,2},{4,5},{5,4},{6,7},{7,6}} | collective-permute-start | bytes 22020104 | tf_op jit(solution)/shard_map/ppermute | solution.py:334
  425.2 414.5 %collective-permute-start.6 = (bf16[2048,1792]{1,0:T(8,128)(2,1)}, bf16[2048,1792]{1,0:T(8,128)(2,1)}, u32[]{:S(2)}, u32[]{:S(2)}) collective-permute-start(bf16[2048,1792]{1,0:T(8,128)(2,1)} %collective-permute-done.5.refs_3_), channel_id=1, source_target_pairs={{0,2},{1,3},{2,0},{3,1},{4,6},{5,7},{6,4},{7,5}} | collective-permute-start | bytes 22020104 | tf_op jit(solution)/shard_map/ppermute | solution.py:331
  425.7 316.0 %collective-permute-start.13 = (bf16[2048,1792]{1,0:T(8,128)(2,1)}, bf16[2048,1792]{1,0:T(8,128)(2,1)}, u32[]{:S(2)}, u32[]{:S(2)}) collective-permute-start(bf16[2048,1792]{1,0:T(8,128)(2,1)} %collective-permute-done.12.refs_4_), channel_id=1, source_target_pairs={{0,1},{1,0},{2,3},{3,2},{4,5},{5,4},{6,7},{7,6}} | collective-permute-start | bytes 22020104 | tf_op jit(solution)/shard_map/ppermute | solution.py:334
  545.2 296.0 %collective-permute-start.10 = (bf16[2048,1792]{1,0:T(8,128)(2,1)}, bf16[2048,1792]{1,0:T(8,128)(2,1)}, u32[]{:S(2)}, u32[]{:S(2)}) collective-permute-start(bf16[2048,1792]{1,0:T(8,128)(2,1)} %collective-permute-done.9.refs_3_), channel_id=1, source_target_pairs={{0,1},{1,0},{2,3},{3,2},{4,5},{5,4},{6,7},{7,6}} | collective-permute-start | bytes 22020104 | tf_op jit(solution)/shard_map/ppermute | solution.py:334
  740.2 388.0 %collective-permute-start.23 = (bf16[16,448,768]{2,1,0:T(8,128)(2,1)}, bf16[16,448,768]{2,1,0:T(8,128)(2,1)}, u32[]{:S(2)}, u32[]{:S(2)}) collective-permute-start(bf16[16,448,768]{2,1,0:T(8,128)(2,1)} %pad_maximum_fusion.1), channel_id=1, source_target_pairs={{0,4},{4,0},{1,5},{5,1},{2,6},{6,2},{3,7},{7,3}} | collective-permute-start | bytes 33030152 | tf_op jit(solution)/shard_map/ppermute | solution.py:328
  741.7 474.2 %collective-permute-start.22 = (bf16[16,448,768]{2,1,0:T(8,128)(2,1)}, bf16[16,448,768]{2,1,0:T(8,128)(2,1)}, u32[]{:S(2)}, u32[]{:S(2)}) collective-permute-start(bf16[16,448,768]{2,1,0:T(8,128)(2,1)} %pad_maximum_fusion), channel_id=1, source_target_pairs={{0,4},{4,0},{1,5},{5,1},{2,6},{6,2},{3,7},{7,3}} | collective-permute-start | bytes 33030152 | tf_op jit(solution)/shard_map/ppermute | solution.py:328
  839.7 494.3 %collective-permute-start.21 = (bf16[8,448,768]{2,1,0:T(8,128)(2,1)}, bf16[8,448,768]{2,1,0:T(8,128)(2,1)}, u32[]{:S(2)}, u32[]{:S(2)}) collective-permute-start(bf16[8,448,768]{2,1,0:T(8,128)(2,1)} %pad_maximum_fusion.7), channel_id=1, source_target_pairs={{0,4},{4,0},{1,5},{5,1},{2,6},{6,2},{3,7},{7,3}} | collective-permute-start | bytes 16515080 | tf_op jit(solution)/shard_map/ppermute | solution.py:328
  990.0 461.4 %collective-permute-start.20 = (bf16[8,448,768]{2,1,0:T(8,128)(2,1)}, bf16[8,448,768]{2,1,0:T(8,128)(2,1)}, u32[]{:S(2)}, u32[]{:S(2)}) collective-permute-start(bf16[8,448,768]{2,1,0:T(8,128)(2,1)} %pad_maximum_fusion.6), channel_id=1, source_target_pairs={{0,4},{4,0},{1,5},{5,1},{2,6},{6,2},{3,7},{7,3}} | collective-permute-start | bytes 16515080 | tf_op jit(solution)/shard_map/ppermute | solution.py:328
  1127.9 369.1 %collective-permute-start.33 = (bf16[16,4,80,896]{3,2,1,0:T(8,128)(2,1)}, bf16[16,4,80,896]{3,2,1,0:T(8,128)(2,1)}, u32[]{:S(2)}, u32[]{:S(2)}) collective-permute-start(bf16[16,4,80,896]{3,2,1,0:T(8,128)(2,1)} %get-tuple-element.139), channel_id=1, source_target_pairs={{0,1},{1,0},{2,3},{3,2},{4,5},{5,4},{6,7},{7,6}} | collective-permute-start | bytes 27525128 | tf_op jit(solution)/shard_map/ppermute | solution.py:334
  1128.2 368.4 %collective-permute-start.34 = (f32[16,4,80,128]{3,2,1,0:T(8,128)}, f32[16,4,80,128]{3,2,1,0:T(8,128)}, u32[]{:S(2)}, u32[]{:S(2)}) collective-permute-start(f32[16,4,80,128]{3,2,1,0:T(8,128)} %get-tuple-element.141), channel_id=1, source_target_pairs={{0,1},{1,0},{2,3},{3,2},{4,5},{5,4},{6,7},{7,6}} | collective-permute-start | bytes 7864328 | tf_op jit(solution)/shard_map/ppermute | solution.py:334
  1216.0 335.4 %collective-permute-start.31 = (bf16[16,4,80,896]{3,2,1,0:T(8,128)(2,1)}, bf16[16,4,80,896]{3,2,1,0:T(8,128)(2,1)}, u32[]{:S(2)}, u32[]{:S(2)}) collective-permute-start(bf16[16,4,80,896]{3,2,1,0:T(8,128)(2,1)} %get-tuple-element.135), channel_id=1, source_target_pairs={{0,1},{1,0},{2,3},{3,2},{4,5},{5,4},{6,7},{7,6}} | collective-permute-start | bytes 27525128 | tf_op jit(solution)/shard_map/ppermute | solution.py:334
  1333.9 216.9 %collective-permute-start.32 = (f32[16,4,80,128]{3,2,1,0:T(8,128)}, f32[16,4,80,128]{3,2,1,0:T(8,128)}, u32[]{:S(2)}, u32[]{:S(2)}) collective-permute-start(f32[16,4,80,128]{3,2,1,0:T(8,128)} %get-tuple-element.137), channel_id=1, source_target_pairs={{0,1},{1,0},{2,3},{3,2},{4,5},{5,4},{6,7},{7,6}} | collective-permute-start | bytes 7864328 | tf_op jit(solution)/shard_map/ppermute | solution.py:334
  1713.2 321.8 %collective-permute-start.35 = (f32[1,2048,896]{2,1,0:T(8,128)}, f32[1,2048,896]{2,1,0:T(8,128)}, u32[]{:S(2)}, u32[]{:S(2)}) collective-permute-start(f32[1,2048,896]{2,1,0:T(8,128)} %get-tuple-element.143), channel_id=1, source_target_pairs={{0,2},{1,3},{2,0},{3,1},{4,6},{5,7},{6,4},{7,5}} | collective-permute-start | bytes 22020104 | tf_op jit(solution)/shard_map/ppermute | solution.py:331
  1727.1 313.8 %collective-permute-start.36 = (f32[1,2048,896]{2,1,0:T(8,128)}, f32[1,2048,896]{2,1,0:T(8,128)}, u32[]{:S(2)}, u32[]{:S(2)}) collective-permute-start(f32[1,2048,896]{2,1,0:T(8,128)} %get-tuple-element.145), channel_id=1, source_target_pairs={{0,2},{1,3},{2,0},{3,1},{4,6},{5,7},{6,4},{7,5}} | collective-permute-start | bytes 22020104 | tf_op jit(solution)/shard_map/ppermute | solution.py:331
  1728.2 304.5 %collective-permute-start.37 = (f32[1,8,2048]{2,1,0:T(8,128)S(1)}, f32[1,8,2048]{2,1,0:T(8,128)S(1)}, u32[]{:S(2)}, u32[]{:S(2)}) collective-permute-start(f32[1,8,2048]{2,1,0:T(8,128)S(1)} %copy-done.12), channel_id=1, source_target_pairs={{0,2},{1,3},{2,0},{3,1},{4,6},{5,7},{6,4},{7,5}} | collective-permute-start | bytes 196616 | tf_op jit(solution)/shard_map/ppermute | solution.py:331
  1729.1 304.4 %collective-permute-start.38 = (f32[1,8,2048]{2,1,0:T(8,128)}, f32[1,8,2048]{2,1,0:T(8,128)S(1)}, u32[]{:S(2)}, u32[]{:S(2)}) collective-permute-start(f32[1,8,2048]{2,1,0:T(8,128)} %get-tuple-element.149), channel_id=1, source_target_pairs={{0,2},{1,3},{2,0},{3,1},{4,6},{5,7},{6,4},{7,5}} | collective-permute-start | bytes 196616 | tf_op jit(solution)/shard_map/ppermute | solution.py:331
  (28 other events, 1921.5 us)
